TPU v7x, 32 devices: a whole 2x2x4 slice. The times are simulated.
32 devices in a mesh: groups: 2 (over x), seq: 16 (over z, y, core).
Axes of the slice: x: 2, y: 2, z: 4, core: 2. Of those that a mesh axis runs over, the one named last changes fastest.
Arguments:
- queries: bfloat16 [8192, 4096], P(('groups', 'seq')), parts along dimension 0, may hold values from -6 to 6
- keys: bfloat16 [8192, 2048], P(('groups', 'seq')), parts along dimension 0, may hold values from -6 to 6
- values: bfloat16 [8192, 2048], P(('groups', 'seq')), parts along dimension 0, may hold values from -6 to 6
- doc_blocks: int32 [16], P('groups'), parts along dimension 0, may hold values from 1 to 8, 32 in all
Outputs:
- attended: bfloat16 [8192, 4096], P(('groups', 'seq')), parts along dimension 0
There are 2 independent parts, one for each index of `groups`. A program takes and returns all parts, laid end to end along the dimension named above; each array names one. Nothing has to cross between parts.
Inputs may be any that keep to these rules, and one draw needn't show every extreme that they name: `doc_blocks`: the lengths add up to 32; the longest document has exactly 8 units.
All inputs are finite; a program needn't handle non-finite values.
Results may differ from a plain program's by a relative error of at most 0.004.
Values may be sent and summed in bfloat16 or wider, within the bound.
No kernel may reach another device: no remote copies, remote signals or barrier semaphores. Data moves between devices by JAX's collectives and lax.ppermute only.
A program may use at most 64 MiB of HBM per device.

v0:
```python
import jax
import jax.numpy as jnp
from jax import lax
from jax.sharding import PartitionSpec as P

DH = 128
BLK = 128
score_scale = 144.0 ** (-0.5)


def from_partner(block, axis, bit):
    count = lax.axis_size(axis)
    route = []
    for low in range(count):
        high = low | 1 << bit
        if high != low and high < count:
            route += [(low, high), (high, low)]
    return lax.ppermute(block, axis, route)


def attend(
    query_heads, query_pos, all_keys, all_values, key_first, doc_blocks, query_block, key_block
):
    query_rows = query_heads.shape[0]
    key_here = query_heads.shape[1]
    ratio = query_heads.shape[2]
    lengths = doc_blocks * BLK
    doc_ends = jnp.cumsum(lengths)
    doc_starts = doc_ends - lengths
    doc_number = jnp.sum((query_pos[:, None] >= doc_ends[None, :]).astype(jnp.int32), axis=1)
    doc_ids = jnp.arange(doc_blocks.shape[0], dtype=jnp.int32)
    own_start = jnp.sum(
        jnp.where(doc_number[:, None] == doc_ids[None, :], doc_starts[None, :], 0), axis=1
    )

    def one_block(block_index):
        first_row = block_index * query_block
        query_tile = lax.dynamic_slice_in_dim(query_heads, first_row, query_block, 0)
        tile_pos = lax.dynamic_slice_in_dim(query_pos, first_row, query_block, 0)
        tile_start = lax.dynamic_slice_in_dim(own_start, first_row, query_block, 0)
        low_block = (tile_start[0] - key_first) // key_block
        high_block = (tile_pos[query_block - 1] - key_first) // key_block + 1
        state_shape = (key_here, ratio, query_block)
        start_state = (
            jnp.full(state_shape, -1e30, jnp.float32),
            jnp.zeros(state_shape, jnp.float32),
            jnp.zeros(state_shape + (DH,), jnp.float32),
        )

        def key_step(key_index, carried):
            run_max, run_total, run_sum = carried
            key_tile = lax.dynamic_slice_in_dim(all_keys, key_index * key_block, key_block, 0)
            value_tile = lax.dynamic_slice_in_dim(all_values, key_index * key_block, key_block, 0)
            scores = (
                jnp.einsum(
                    "qgsd,kgd->gsqk", query_tile, key_tile, preferred_element_type=jnp.float32
                )
                * score_scale
            )
            key_pos = key_first + key_index * key_block + jnp.arange(key_block, dtype=jnp.int32)
            visible = (key_pos[None, :] >= tile_start[:, None]) & (
                key_pos[None, :] <= tile_pos[:, None]
            )
            masked = jnp.where(visible, scores, -1e30)
            new_max = jnp.maximum(run_max, jnp.max(masked, axis=-1))
            rescale = jnp.exp(run_max - new_max)
            weights = jnp.where(visible, jnp.exp(scores - new_max[..., None]), 0.0)
            run_total = run_total * rescale + jnp.sum(weights, axis=-1)
            run_sum = run_sum * rescale[..., None] + jnp.einsum(
                "gsqk,kgd->gsqd",
                weights.astype(jnp.bfloat16),
                value_tile,
                preferred_element_type=jnp.float32,
            )
            return (new_max, run_total, run_sum)

        finished = lax.fori_loop(low_block, high_block, key_step, start_state)
        blended = finished[2] / finished[1][..., None]
        return (
            blended.transpose(2, 0, 1, 3)
            .reshape(query_block, key_here * ratio * DH)
            .astype(jnp.bfloat16)
        )

    blocks = lax.map(one_block, jnp.arange(query_rows // query_block, dtype=jnp.int32))
    return blocks.reshape(query_rows, key_here * ratio * DH)


def on_device(queries, keys, values, doc_blocks):
    axis_size = lax.axis_size("seq")
    my_index = lax.axis_index("seq")
    shard_rows = queries.shape[0]
    head_count = queries.shape[1] // DH
    key_count = keys.shape[1] // DH
    group_ratio = head_count // key_count
    total_rows = shard_rows * axis_size
    heads_here = max(1, head_count // axis_size)
    row_split = max(1, axis_size // head_count)
    head_groups = head_count // heads_here
    key_here = max(1, heads_here // group_ratio)
    key_groups = key_count // key_here
    copies = axis_size // key_groups
    part_rows = shard_rows // row_split
    query_width = heads_here * DH
    key_width = key_here * DH
    outgoing = queries.reshape(row_split, part_rows, head_groups, query_width).transpose(2, 0, 1, 3)
    outgoing = outgoing.reshape(axis_size, part_rows, query_width)
    got_queries = lax.all_to_all(outgoing, "seq", split_axis=0, concat_axis=0, tiled=True)
    piece_rows = shard_rows // copies
    stacked = jnp.stack((keys, values)).reshape(2, copies, piece_rows, key_groups, key_width)
    stacked = stacked.transpose(0, 3, 1, 2, 4).reshape(2, axis_size, piece_rows, key_width)
    got_pairs = lax.all_to_all(stacked, "seq", split_axis=1, concat_axis=1, tiled=True)
    gathered = got_pairs.reshape(2, axis_size, 1, piece_rows, key_width)
    for bit_number in range(copies.bit_length() - 1):
        partner = from_partner(gathered, "seq", bit_number)
        upper_half = my_index // 2**bit_number % 2 == 1
        gathered = jnp.where(
            upper_half,
            jnp.concatenate((partner, gathered), axis=2),
            jnp.concatenate((gathered, partner), axis=2),
        )
    pairs_flat = gathered.reshape(2, total_rows, key_here, DH)
    all_keys = pairs_flat[0]
    all_values = pairs_flat[1]
    query_rows = total_rows // row_split
    row_ids = jnp.arange(query_rows, dtype=jnp.int32)
    my_part = my_index % row_split
    query_pos = row_ids // part_rows * shard_rows + my_part * part_rows + row_ids % part_rows
    query_heads = got_queries.reshape(query_rows, key_here, heads_here // key_here, DH)
    result = attend(
        query_heads,
        query_pos,
        all_keys,
        all_values,
        0,
        doc_blocks,
        min(512, query_rows),
        min(512, total_rows),
    )
    result_parts = result.reshape(axis_size, part_rows, query_width)
    returned = lax.all_to_all(result_parts, "seq", split_axis=0, concat_axis=0, tiled=True)
    returned = returned.reshape(head_groups, row_split, part_rows, query_width).transpose(
        1, 2, 0, 3
    )
    return returned.reshape(shard_rows, head_count * DH)


def solution(mesh):
    in_specs = (
        P(("groups", "seq"), None),
        P(("groups", "seq"), None),
        P(("groups", "seq"), None),
        P("groups"),
    )
    out_specs = P(("groups", "seq"), None)
    return jax.shard_map(
        on_device, mesh=mesh, in_specs=in_specs, out_specs=out_specs, check_vma=False
    )
```

profile of v0, /device:TPU:11, one launch (start us, length us, event | category | flops | bytes accessed | tf_op | source)
XLA Modules:
  0.0 290.4 jit_solution(64911163191725977)
XLA Ops:
  0.0 4.1 %copy.34 = bf16[256,4096]{0,1:T(8,128)(2,1)} copy(bf16[256,4096]{1,0:T(8,128)(2,1)} %param.8) | data formatting | bytes 4194304 | tf_op args[0]
  4.1 6.6 %all-to-all-start = ((bf16[16,256,256]{1,2,0:T(8,128)(2,1)}), bf16[16,256,256]{1,2,0:T(8,128)(2,1)S(1)}, u32[]{:S(2)}, u32[]{:S(2)}) async-start(bf16[16,256,256]{1,2,0:T(8,128)(2,1)} %bitcast.116), calls=%async_computation | async-start | bytes 4194304 | tf_op jit(solution)/shard_map/all_to_all | solution.py:108
  10.6 1.5 copy.36
  12.1 2.3 copy.37
  14.4 2.8 maximum_bitcast_fusion
  17.2 4.0 %copy.38 = bf16[2,16,256,128]{3,2,0,1:T(8,128)(2,1)} copy(bf16[2,16,256,128]{2,3,1,0:T(8,128)(2,1)} %maximum_bitcast_fusion) | data formatting | bytes 4194304 | tf_op jit(solution)/shard_map/reshape | solution.py:111
  21.1 35.6 %all-to-all-done = bf16[16,256,256]{1,2,0:T(8,128)(2,1)S(1)} async-done(((bf16[16,256,256]{1,2,0:T(8,128)(2,1)}), bf16[16,256,256]{1,2,0:T(8,128)(2,1)S(1)}, u32[]{:S(2)}, u32[]{:S(2)}) %all-to-all-start) | async-done | bytes 2097184 | tf_op jit(solution)/shard_map/all_to_all | solution.py:108
  56.7 6.1 %all-to-all-start.1 = ((bf16[2,16,256,128]{3,2,0,1:T(8,128)(2,1)}), bf16[2,16,256,128]{3,2,0,1:T(8,128)(2,1)}, u32[]{:S(2)}, u32[]{:S(2)}) async-start(bf16[2,16,256,128]{3,2,0,1:T(8,128)(2,1)} %copy.38), calls=%async_computation.1 | async-start | bytes 4194304 | tf_op jit(solution)/shard_map/all_to_all | solution.py:112
  63.3 2.5 copy.35
  65.8 4.2 %reshape.133 = bf16[4096,1,2,128]{0,3,2,1:T(8,128)(2,1)} reshape(bf16[16,256,256]{1,0,2:T(8,128)(2,1)} %copy.35) | data formatting | bytes 4194304 | tf_op jit(solution)/shard_map/reshape | solution.py:129
  70.0 39.0 %all-to-all-done.1 = bf16[2,16,256,128]{3,2,0,1:T(8,128)(2,1)} async-done(((bf16[2,16,256,128]{3,2,0,1:T(8,128)(2,1)}), bf16[2,16,256,128]{3,2,0,1:T(8,128)(2,1)}, u32[]{:S(2)}, u32[]{:S(2)}) %all-to-all-start.1) | async-done | bytes 2097184 | tf_op jit(solution)/shard_map/all_to_all | solution.py:112
  109.0 1.7 fusion.33
  110.8 119.2 %while.44 = (s32[]{:T(128)}, bf16[8,512,256]{2,1,0:T(8,128)(2,1)}, s32[8]{0:T(128)S(1)}, s32[4096]{0:T(1024)S(1)}, s32[4096]{0:T(1024)S(1)}, /*index=5*/bf16[409...) while((s32[]{:T(128)}, bf16[8,512,256]{2,1,0:T(8,128)(2,1)}, ...), condition=%wide.region_8.9_spmd, body=%wide.region_3.8_spmd.sunk | while | flops 275516960 | bytes 12940678 | solution.py:85
  118.2 1.0 constant_dynamic-slice_fusion.2
  119.5 2.3 while.45
  120.4 0.8 fusion.47
  130.6 1.0 constant_dynamic-slice_fusion.2
  131.8 4.5 %while.45 = (s32[]{:T(128)}, f32[1,2,512]{2,1,0:T(2,128)S(1)}, f32[1,2,512]{2,1,0:T(2,128)S(1)}, f32[1,2,512,128]{3,2,1,0:T(8,128)S(1)}, s32[]{:T(128)}, /*index...) while((s32[]{:T(128)}, f32[1,2,512]{2,1,0:T(2,128)S(1)}, ...), condition=%wide.region_7.7_spmd, body=%wide.region_4.6_spmd.sunk | while | flops 275254784 | bytes 8986815 | solution.py:77
  132.7 0.8 fusion.47
  135.0 0.8 fusion.47
  145.2 1.0 constant_dynamic-slice_fusion.2
  146.4 4.5 %while.45 = (s32[]{:T(128)}, f32[1,2,512]{2,1,0:T(2,128)S(1)}, f32[1,2,512]{2,1,0:T(2,128)S(1)}, f32[1,2,512,128]{3,2,1,0:T(8,128)S(1)}, s32[]{:T(128)}, /*index...) while((s32[]{:T(128)}, f32[1,2,512]{2,1,0:T(2,128)S(1)}, ...), condition=%wide.region_7.7_spmd, body=%wide.region_4.6_spmd.sunk | while | flops 275254784 | bytes 8986815 | solution.py:77
  147.3 0.8 fusion.47
  149.6 0.8 fusion.47
  159.8 1.0 constant_dynamic-slice_fusion.2
  161.0 6.8 %while.45 = (s32[]{:T(128)}, f32[1,2,512]{2,1,0:T(2,128)S(1)}, f32[1,2,512]{2,1,0:T(2,128)S(1)}, f32[1,2,512,128]{3,2,1,0:T(8,128)S(1)}, s32[]{:T(128)}, /*index...) while((s32[]{:T(128)}, f32[1,2,512]{2,1,0:T(2,128)S(1)}, ...), condition=%wide.region_7.7_spmd, body=%wide.region_4.6_spmd.sunk | while | flops 275254784 | bytes 8986815 | solution.py:77
  161.9 0.8 fusion.47
  164.2 0.8 fusion.47
  166.5 0.8 fusion.47
  176.7 1.0 constant_dynamic-slice_fusion.2
  177.9 4.5 %while.45 = (s32[]{:T(128)}, f32[1,2,512]{2,1,0:T(2,128)S(1)}, f32[1,2,512]{2,1,0:T(2,128)S(1)}, f32[1,2,512,128]{3,2,1,0:T(8,128)S(1)}, s32[]{:T(128)}, /*index...) while((s32[]{:T(128)}, f32[1,2,512]{2,1,0:T(2,128)S(1)}, ...), condition=%wide.region_7.7_spmd, body=%wide.region_4.6_spmd.sunk | while | flops 275254784 | bytes 8986815 | solution.py:77
  178.8 0.8 fusion.47
  181.1 0.8 fusion.47
  191.3 1.0 constant_dynamic-slice_fusion.2
  192.6 4.5 %while.45 = (s32[]{:T(128)}, f32[1,2,512]{2,1,0:T(2,128)S(1)}, f32[1,2,512]{2,1,0:T(2,128)S(1)}, f32[1,2,512,128]{3,2,1,0:T(8,128)S(1)}, s32[]{:T(128)}, /*index...) while((s32[]{:T(128)}, f32[1,2,512]{2,1,0:T(2,128)S(1)}, ...), condition=%wide.region_7.7_spmd, body=%wide.region_4.6_spmd.sunk | while | flops 275254784 | bytes 8986815 | solution.py:77
  193.4 0.8 fusion.47
  195.7 0.8 fusion.47
  206.0 1.0 constant_dynamic-slice_fusion.2
  207.2 4.5 %while.45 = (s32[]{:T(128)}, f32[1,2,512]{2,1,0:T(2,128)S(1)}, f32[1,2,512]{2,1,0:T(2,128)S(1)}, f32[1,2,512,128]{3,2,1,0:T(8,128)S(1)}, s32[]{:T(128)}, /*index...) while((s32[]{:T(128)}, f32[1,2,512]{2,1,0:T(2,128)S(1)}, ...), condition=%wide.region_7.7_spmd, body=%wide.region_4.6_spmd.sunk | while | flops 275254784 | bytes 8986815 | solution.py:77
  208.1 0.8 fusion.47
  210.3 0.8 fusion.47
  220.6 1.0 constant_dynamic-slice_fusion.2
  221.8 6.8 %while.45 = (s32[]{:T(128)}, f32[1,2,512]{2,1,0:T(2,128)S(1)}, f32[1,2,512]{2,1,0:T(2,128)S(1)}, f32[1,2,512,128]{3,2,1,0:T(8,128)S(1)}, s32[]{:T(128)}, /*index...) while((s32[]{:T(128)}, f32[1,2,512]{2,1,0:T(2,128)S(1)}, ...), condition=%wide.region_7.7_spmd, body=%wide.region_4.6_spmd.sunk | while | flops 275254784 | bytes 8986815 | solution.py:77
  222.7 0.8 fusion.47
  224.9 0.8 fusion.47
  230.0 53.9 %all_to_all.15 = bf16[16,256,256]{2,1,0:T(8,128)(2,1)S(1)} all-to-all(bf16[16,256,256]{2,1,0:T(8,128)(2,1)} %bitcast.121), channel_id=1, replica_groups=mesh['groups'=2,'seq'=16] {'seq'}, dimensions={0} | all-to-all | bytes 4194304 | tf_op jit(solution)/shard_map/all_to_all | solution.py:141
  283.9 2.4 copy.40
  286.3 4.1 %copy.41 = bf16[256,4096]{1,0:T(8,128)(2,1)} copy(bf16[256,4096]{0,1:T(8,128)(2,1)} %bitcast.117) | data formatting | bytes 4194304 | tf_op jit(solution)/shard_map/reshape | solution.py:145
  (234 shorter events, 52.1 us)
Async XLA Ops:
  4.1 52.7 %all-to-all-start = ((bf16[16,256,256]{1,2,0:T(8,128)(2,1)}), bf16[16,256,256]{1,2,0:T(8,128)(2,1)S(1)}, u32[]{:S(2)}, u32[]{:S(2)}) async-start(bf16[16,256,256]{1,2,0:T(8,128)(2,1)} %bitcast.116), calls=%async_computation | async-start | bytes 4194304 | tf_op jit(solution)/shard_map/all_to_all | solution.py:108
  21.1 41.7 %copy-start = (s32[8]{0:T(128)S(1)}, s32[8]{0:T(128)}, u32[]{:S(2)}) copy-start(s32[8]{0:T(128)} %param.11) | copy-start | bytes 100
  56.7 52.3 %all-to-all-start.1 = ((bf16[2,16,256,128]{3,2,0,1:T(8,128)(2,1)}), bf16[2,16,256,128]{3,2,0,1:T(8,128)(2,1)}, u32[]{:S(2)}, u32[]{:S(2)}) async-start(bf16[2,16,256,128]{3,2,0,1:T(8,128)(2,1)} %copy.38), calls=%async_computation.1 | async-start | bytes 4194304 | tf_op jit(solution)/shard_map/all_to_all | solution.py:112
where the time goes:
time: 292 us; the launch traced here: 290 us
  waiting for transfers between devices  74.6 us (26%)
  local copies, waits for them, and re-layouts  60.7 us (21%)
  blocking collectives  53.9 us (18%)
  loops' own time  46.3 us (16%)
  matrix products  23.7 us (8%)
  other arithmetic  18.4 us (6%)
  starting transfers between devices  12.7 us (4%)
    all_to_all x1, blocking collectives, on_device(): lax.all_to_all(result_parts, 'seq', split_axis=0, concat_axis=0, tiled=True)  53.9 us
    another operation x1, loops' own time, attend(): lax.map(one_block, jnp.arange(query_rows // query_block, dtype=jnp.int32))  45 us
    all_to_all x1, waiting for transfers between devices, on_device(): lax.all_to_all(stacked, 'seq', split_axis=1, concat_axis=1, tiled=True)  39 us
    all_to_all x1, waiting for transfers between devices, on_device(): lax.all_to_all(outgoing, 'seq', split_axis=0, concat_axis=0, tiled=True)  35.6 us
    dot_general x17, matrix products, key_step(): jnp.einsum('gsqk,kgd->gsqd', weights.astype(jnp.bfloat16), value_tile, pr...  14.3 us
    dot_general x17, matrix products, key_step(): jnp.einsum('qgsd,kgd->gsqk', query_tile, key_tile, preferred_element_type...  9.37 us
    dynamic_slice x16, local copies, waits for them, and re-layouts, one_block(): lax.dynamic_slice_in_dim(query_heads, first_row, query_block, 0)  9.15 us
    reduce_sum x17, other arithmetic, key_step(): run_total = run_total * rescale + jnp.sum(weights, axis=-1)  8.43 us
  transfers between devices with their start and end apart: 2, of which 2 were waited for; matrix products, arithmetic and copies ran while one was open for 6% of the time, Pallas kernels for 0%

commit v1 on v0

--- a/solution.py
+++ b/solution.py
@@ -109,7 +109,16 @@
     piece_rows = shard_rows // copies
     stacked = jnp.stack((keys, values)).reshape(2, copies, piece_rows, key_groups, key_width)
     stacked = stacked.transpose(0, 3, 1, 2, 4).reshape(2, axis_size, piece_rows, key_width)
-    got_pairs = lax.all_to_all(stacked, "seq", split_axis=1, concat_axis=1, tiled=True)
+
+    def waves_cut(tile_in, d0, along_dim):
+        return jnp.concatenate(
+            lax.all_to_all(
+                jnp.stack(jnp.split(tile_in, lax.axis_size("seq"), axis=d0), axis=0), "seq", 0, 0
+            ),
+            axis=along_dim,
+        )
+
+    got_pairs = waves_cut(stacked, 1, 1)
     gathered = got_pairs.reshape(2, axis_size, 1, piece_rows, key_width)
     for bit_number in range(copies.bit_length() - 1):
         partner = from_partner(gathered, "seq", bit_number)

time: 292 us -> 312 us (1.068)
  matrix products: 23.7 us -> 39.1 us
  waiting for transfers between devices: 74.6 us -> 86.6 us
  local copies, waits for them, and re-layouts: 60.7 us -> 55.4 us
    dot_general x17, matrix products: 14.3 us -> 29.7 us  [key_step(): jnp.einsum('gsqk,kgd->gsqd', weights.astype(jnp.bfloat16), value_tile, pr...]
    all_to_all x1, waiting for transfers between devices: 35.6 us -> 44.6 us  [on_device(): lax.all_to_all(outgoing, 'seq', split_axis=0, concat_axis=0, tiled=True)]
    reshape x1 -> x0, local copies, waits for them, and re-layouts: 3.95 us -> none  [on_device(): stacked.transpose(0, 3, 1, 2, 4)]
    unnamed x5 -> x22, local copies, waits for them, and re-layouts: 7.83 us -> 6.34 us
  transfers between devices with their start and end apart: 2 -> 2, of which waited for: 2 -> 2; matrix products, arithmetic and copies ran while one was open for 6% -> 2% of each run, Pallas kernels for 0% -> 0%
where the time goes in v1:
time: 312 us; the launch traced here: 310 us
  waiting for transfers between devices  86.6 us (28%)
  local copies, waits for them, and re-layouts  55.4 us (18%)
  blocking collectives  53.9 us (17%)
  loops' own time  46.3 us (15%)
  matrix products  39.1 us (13%)
  other arithmetic  15.9 us (5%)
  starting transfers between devices  12.8 us (4%)
    all_to_all x1, blocking collectives, on_device(): lax.all_to_all(result_parts, 'seq', split_axis=0, concat_axis=0, tiled=True)  53.9 us
    another operation x1, loops' own time, attend(): lax.map(one_block, jnp.arange(query_rows // query_block, dtype=jnp.int32))  45 us
    all_to_all x1, waiting for transfers between devices, on_device(): lax.all_to_all(outgoing, 'seq', split_axis=0, concat_axis=0, tiled=True)  44.6 us
    all_to_all x1, waiting for transfers between devices, waves_cut(): lax.all_to_all(jnp.stack(jnp.split(tile_in, lax.axis_size('seq'), axis=d0...  42 us
    dot_general x17, matrix products, key_step(): jnp.einsum('gsqk,kgd->gsqd', weights.astype(jnp.bfloat16), value_tile, pr...  29.7 us
    dot_general x17, matrix products, key_step(): jnp.einsum('qgsd,kgd->gsqk', query_tile, key_tile, preferred_element_type...  9.38 us
    dynamic_slice x16, local copies, waits for them, and re-layouts, one_block(): lax.dynamic_slice_in_dim(query_heads, first_row, query_block, 0)  9.15 us
    reduce_sum x17, other arithmetic, key_step(): run_total = run_total * rescale + jnp.sum(weights, axis=-1)  8.43 us
  transfers between devices with their start and end apart: 2, of which 2 were waited for; matrix products, arithmetic and copies ran while one was open for 2% of the time, Pallas kernels for 0%

profile of v1, /device:TPU:11, one launch (start us, length us, event | category | flops | bytes accessed | tf_op | source)
XLA Modules:
  0.0 310.2 jit_solution(16234062451891943363)
XLA Ops:
  0.0 1.6 copy.96
  2.6 2.4 copy.113
  5.0 6.6 %all-to-all-start.1 = ((bf16[16,2,1,256,128]{4,3,2,1,0:T(8,128)(2,1)}), bf16[16,2,1,256,128]{4,3,2,1,0:T(8,128)(2,1)S(1)}, u32[]{:S(2)}, u32[]{:S(2)}) async-start(bf16[16,2,1,256,128]{4,3,2,1,0:T(8,128)(2,1)} %copy.113), calls=%async_computation.1 | async-start | bytes 4194304 | tf_op jit(solution)/shard_map/all_to_all | solution.py:115
  11.6 4.1 %copy.94 = bf16[256,4096]{0,1:T(8,128)(2,1)} copy(bf16[256,4096]{1,0:T(8,128)(2,1)} %param.8) | data formatting | bytes 4194304 | tf_op args[0]
  15.7 42.0 %all-to-all-done.1 = bf16[16,2,1,256,128]{4,3,2,1,0:T(8,128)(2,1)S(1)} async-done(((bf16[16,2,1,256,128]{4,3,2,1,0:T(8,128)(2,1)}), bf16[16,2,1,256,128]{4,3,2,1,0:T(8,128)(2,1)S(1)}, u32[]{:S(2)}, u32[]{:S(2)}) %all-to-all-start.1) | async-done | bytes 2097184 | tf_op jit(solution)/shard_map/all_to_all | solution.py:115
  57.7 6.2 %all-to-all-start = ((bf16[16,256,256]{1,2,0:T(8,128)(2,1)}), bf16[16,256,256]{1,2,0:T(8,128)(2,1)}, u32[]{:S(2)}, u32[]{:S(2)}) async-start(bf16[16,256,256]{1,2,0:T(8,128)(2,1)} %bitcast.212), calls=%async_computation | async-start | bytes 4194304 | tf_op jit(solution)/shard_map/all_to_all | solution.py:108
  64.4 1.1 fusion.49
  65.5 44.6 %all-to-all-done = bf16[16,256,256]{1,2,0:T(8,128)(2,1)} async-done(((bf16[16,256,256]{1,2,0:T(8,128)(2,1)}), bf16[16,256,256]{1,2,0:T(8,128)(2,1)}, u32[]{:S(2)}, u32[]{:S(2)}) %all-to-all-start) | async-done | bytes 2097184 | tf_op jit(solution)/shard_map/all_to_all | solution.py:108
  110.1 2.8 copy.95
  112.9 2.4 reshape.136
  115.2 134.6 %while.44 = (s32[]{:T(128)}, bf16[8,512,256]{2,1,0:T(8,128)(2,1)}, s32[8]{0:T(128)S(1)}, s32[4096]{0:T(1024)S(1)}, s32[4096]{0:T(1024)S(1)}, /*index=5*/bf16[409...) while((s32[]{:T(128)}, bf16[8,512,256]{2,1,0:T(8,128)(2,1)}, ...), condition=%wide.region_8.9_spmd, body=%wide.region_3.8_spmd.sunk | while | flops 275516960 | bytes 12940678 | solution.py:85
  122.7 1.0 constant_dynamic-slice_fusion.2
  123.9 3.2 %while.45 = (s32[]{:T(128)}, f32[1,2,512]{2,1,0:T(2,128)S(1)}, f32[1,2,512]{2,1,0:T(2,128)S(1)}, f32[1,2,512,128]{3,2,1,0:T(8,128)S(1)}, s32[]{:T(128)}, /*index...) while((s32[]{:T(128)}, f32[1,2,512]{2,1,0:T(2,128)S(1)}, ...), condition=%wide.region_7.7_spmd, body=%wide.region_4.6_spmd.sunk | while | flops 275254784 | bytes 8986815 | solution.py:77
  124.8 1.7 fusion.63
  127.8 0.7 constant_dynamic-update-slice_fusion.2
  136.0 1.0 constant_dynamic-slice_fusion.2
  137.2 6.4 %while.45 = (s32[]{:T(128)}, f32[1,2,512]{2,1,0:T(2,128)S(1)}, f32[1,2,512]{2,1,0:T(2,128)S(1)}, f32[1,2,512,128]{3,2,1,0:T(8,128)S(1)}, s32[]{:T(128)}, /*index...) while((s32[]{:T(128)}, f32[1,2,512]{2,1,0:T(2,128)S(1)}, ...), condition=%wide.region_7.7_spmd, body=%wide.region_4.6_spmd.sunk | while | flops 275254784 | bytes 8986815 | solution.py:77
  138.1 1.7 fusion.63
  141.2 1.7 fusion.63
  152.4 1.0 constant_dynamic-slice_fusion.2
  153.6 6.4 %while.45 = (s32[]{:T(128)}, f32[1,2,512]{2,1,0:T(2,128)S(1)}, f32[1,2,512]{2,1,0:T(2,128)S(1)}, f32[1,2,512,128]{3,2,1,0:T(8,128)S(1)}, s32[]{:T(128)}, /*index...) while((s32[]{:T(128)}, f32[1,2,512]{2,1,0:T(2,128)S(1)}, ...), condition=%wide.region_7.7_spmd, body=%wide.region_4.6_spmd.sunk | while | flops 275254784 | bytes 8986815 | solution.py:77
  154.5 1.7 fusion.63
  157.7 1.7 fusion.63
  168.8 1.0 constant_dynamic-slice_fusion.2
  170.0 9.5 %while.45 = (s32[]{:T(128)}, f32[1,2,512]{2,1,0:T(2,128)S(1)}, f32[1,2,512]{2,1,0:T(2,128)S(1)}, f32[1,2,512,128]{3,2,1,0:T(8,128)S(1)}, s32[]{:T(128)}, /*index...) while((s32[]{:T(128)}, f32[1,2,512]{2,1,0:T(2,128)S(1)}, ...), condition=%wide.region_7.7_spmd, body=%wide.region_4.6_spmd.sunk | while | flops 275254784 | bytes 8986815 | solution.py:77
  170.9 1.7 fusion.63
  174.1 1.7 fusion.63
  177.3 1.7 fusion.63
  188.4 1.0 constant_dynamic-slice_fusion.2
  189.6 6.4 %while.45 = (s32[]{:T(128)}, f32[1,2,512]{2,1,0:T(2,128)S(1)}, f32[1,2,512]{2,1,0:T(2,128)S(1)}, f32[1,2,512,128]{3,2,1,0:T(8,128)S(1)}, s32[]{:T(128)}, /*index...) while((s32[]{:T(128)}, f32[1,2,512]{2,1,0:T(2,128)S(1)}, ...), condition=%wide.region_7.7_spmd, body=%wide.region_4.6_spmd.sunk | while | flops 275254784 | bytes 8986815 | solution.py:77
  190.5 1.7 fusion.63
  193.7 1.7 fusion.63
  204.9 1.0 constant_dynamic-slice_fusion.2
  206.1 6.4 %while.45 = (s32[]{:T(128)}, f32[1,2,512]{2,1,0:T(2,128)S(1)}, f32[1,2,512]{2,1,0:T(2,128)S(1)}, f32[1,2,512,128]{3,2,1,0:T(8,128)S(1)}, s32[]{:T(128)}, /*index...) while((s32[]{:T(128)}, f32[1,2,512]{2,1,0:T(2,128)S(1)}, ...), condition=%wide.region_7.7_spmd, body=%wide.region_4.6_spmd.sunk | while | flops 275254784 | bytes 8986815 | solution.py:77
  207.0 1.7 fusion.63
  210.1 1.7 fusion.63
  221.3 1.0 constant_dynamic-slice_fusion.2
  222.5 6.4 %while.45 = (s32[]{:T(128)}, f32[1,2,512]{2,1,0:T(2,128)S(1)}, f32[1,2,512]{2,1,0:T(2,128)S(1)}, f32[1,2,512,128]{3,2,1,0:T(8,128)S(1)}, s32[]{:T(128)}, /*index...) while((s32[]{:T(128)}, f32[1,2,512]{2,1,0:T(2,128)S(1)}, ...), condition=%wide.region_7.7_spmd, body=%wide.region_4.6_spmd.sunk | while | flops 275254784 | bytes 8986815 | solution.py:77
  223.4 1.7 fusion.63
  226.6 1.7 fusion.63
  237.7 1.0 constant_dynamic-slice_fusion.2
  238.9 9.5 %while.45 = (s32[]{:T(128)}, f32[1,2,512]{2,1,0:T(2,128)S(1)}, f32[1,2,512]{2,1,0:T(2,128)S(1)}, f32[1,2,512,128]{3,2,1,0:T(8,128)S(1)}, s32[]{:T(128)}, /*index...) while((s32[]{:T(128)}, f32[1,2,512]{2,1,0:T(2,128)S(1)}, ...), condition=%wide.region_7.7_spmd, body=%wide.region_4.6_spmd.sunk | while | flops 275254784 | bytes 8986815 | solution.py:77
  239.8 1.7 fusion.63
  243.0 1.7 fusion.63
  246.2 1.7 fusion.63
  249.9 53.9 %all_to_all.15 = bf16[16,256,256]{2,1,0:T(8,128)(2,1)S(1)} all-to-all(bf16[16,256,256]{2,1,0:T(8,128)(2,1)} %bitcast.217), channel_id=1, replica_groups=mesh['groups'=2,'seq'=16] {'seq'}, dimensions={0} | all-to-all | bytes 4194304 | tf_op jit(solution)/shard_map/all_to_all | solution.py:150
  303.8 2.4 copy.115
  306.2 4.1 %copy.116 = bf16[256,4096]{1,0:T(8,128)(2,1)} copy(bf16[256,4096]{0,1:T(8,128)(2,1)} %bitcast.213) | data formatting | bytes 4194304 | tf_op jit(solution)/shard_map/reshape | solution.py:154
  (252 shorter events, 51.4 us)
Async XLA Ops:
  0.0 1.6 copy-start
  5.0 52.7 %all-to-all-start.1 = ((bf16[16,2,1,256,128]{4,3,2,1,0:T(8,128)(2,1)}), bf16[16,2,1,256,128]{4,3,2,1,0:T(8,128)(2,1)S(1)}, u32[]{:S(2)}, u32[]{:S(2)}) async-start(bf16[16,2,1,256,128]{4,3,2,1,0:T(8,128)(2,1)} %copy.113), calls=%async_computation.1 | async-start | bytes 4194304 | tf_op jit(solution)/shard_map/all_to_all | solution.py:115
  57.7 6.3 %copy-start.1 = (s32[8]{0:T(128)S(1)}, s32[8]{0:T(128)}, u32[]{:S(2)}) copy-start(s32[8]{0:T(128)} %param.11) | copy-start | bytes 100
  57.7 52.4 %all-to-all-start = ((bf16[16,256,256]{1,2,0:T(8,128)(2,1)}), bf16[16,256,256]{1,2,0:T(8,128)(2,1)}, u32[]{:S(2)}, u32[]{:S(2)}) async-start(bf16[16,256,256]{1,2,0:T(8,128)(2,1)} %bitcast.212), calls=%async_computation | async-start | bytes 4194304 | tf_op jit(solution)/shard_map/all_to_all | solution.py:108
